TPU v7x, 32 devices: a whole 2x2x4 slice. The times are simulated.
32 devices in a mesh: row: 8 (over z, x), col: 4 (over y, core).
Axes of the slice: x: 2, y: 2, z: 4, core: 2. Of those that a mesh axis runs over, the one named last changes fastest.
Arguments:
- voltage: float32 [2, 4096, 16384], P(None, ('row', 'col')), may hold values from -6 to 6
- chirp_phase: float32 [16384, 4096], P(('row', 'col')), may hold values from -3.140625 to 3.140625
- filter_taps: float32 [8, 1024], replicated, may hold values from -0.0625 to 0.0625
Outputs:
- filterbank: float32 [2, 1024, 65536], P(None, None, ('row', 'col'))
All inputs are finite; a program needn't handle non-finite values.
Results may differ from a plain program's by a relative error of at most 0.00015.
Values sent between devices are 32-bit elements; how exact they have to be, the bound alone decides.
No kernel may reach another device: no remote copies, remote signals or barrier semaphores. Data moves between devices by JAX's collectives and lax.ppermute only.
A program may use at most 192 MiB of HBM per device.

v0:
```python
import math
import jax
import jax.numpy as jnp
from jax import lax
from jax.sharding import PartitionSpec as P

precise = lax.Precision.HIGHEST


def passed_along(block, axis, distance):
    devices = range(lax.axis_size(axis))
    route = [(i - distance, i) for i in devices if i - distance in devices]
    return lax.ppermute(block, axis, route)


def dft_table(radix, direction):
    digits = jnp.arange(radix, dtype=jnp.int32)
    product = digits[:, None] * digits[None, :] % radix
    turn = direction * 2.0 * math.pi / radix * product.astype(jnp.float32)
    cos_part = jnp.cos(turn)
    sin_part = jnp.sin(turn)
    upper = jnp.stack([cos_part, sin_part], axis=1)
    lower = jnp.stack([-sin_part, cos_part], axis=1)
    return jnp.stack([upper, lower], axis=0)


def complex_product(values, cos_part, sin_part):
    real_part = values[0] * cos_part - values[1] * sin_part
    imag_part = values[0] * sin_part + values[1] * cos_part
    return jnp.stack([real_part, imag_part])


def inner_twist(outer_radix, inner_radix, direction):
    outer_digits = jnp.arange(outer_radix, dtype=jnp.int32)
    inner_digits = jnp.arange(inner_radix, dtype=jnp.int32)
    length = outer_radix * inner_radix
    product = outer_digits[:, None] * inner_digits[None, :] % length
    turn = direction * 2.0 * math.pi / length * product.astype(jnp.float32)
    return (jnp.cos(turn), jnp.sin(turn))


def dft_rows(values, direction):
    length = values.shape[1]
    column_count = values.shape[2]
    inner_radix = min(length, 128)
    outer_radix = length // inner_radix
    blocked = values.reshape(2, outer_radix, inner_radix, column_count)
    partial_value = jnp.einsum(
        "cadk,cabm->dkbm", dft_table(outer_radix, direction), blocked, precision=precise
    )
    cos_part, sin_part = inner_twist(outer_radix, inner_radix, direction)
    partial_value = complex_product(partial_value, cos_part[:, :, None], sin_part[:, :, None])
    result = jnp.einsum(
        "cbdq,ckbm->dqkm", dft_table(inner_radix, direction), partial_value, precision=precise
    )
    return result.reshape(2, length, column_count)


def dft_cols(values, direction):
    length = values.shape[2]
    row_count = values.shape[1]
    inner_radix = min(length, 128)
    outer_radix = length // inner_radix
    blocked = values.reshape(2, row_count, outer_radix, inner_radix)
    partial_value = jnp.einsum(
        "cadk,cmab->dmkb", dft_table(outer_radix, direction), blocked, precision=precise
    )
    cos_part, sin_part = inner_twist(outer_radix, inner_radix, direction)
    partial_value = complex_product(partial_value, cos_part, sin_part)
    result = jnp.einsum(
        "cbdq,cmkb->dmqk", dft_table(inner_radix, direction), partial_value, precision=precise
    )
    return result.reshape(2, row_count, length)


def rotate(values, row_index, col_index, total, direction, factor):
    product = row_index[:, None] * col_index[None, :] % total
    turn = direction * 2.0 * math.pi / total * product.astype(jnp.float32)
    return complex_product(values, factor * jnp.cos(turn), factor * jnp.sin(turn))


def spread(values):
    return lax.all_to_all(values, ("row", "col"), split_axis=2, concat_axis=1, tiled=True)


def collect(values):
    return lax.all_to_all(values, ("row", "col"), split_axis=1, concat_axis=2, tiled=True)


def local(voltage, chirp_phase, filter_taps):
    device_count = lax.axis_size("row") * lax.axis_size("col")
    device = lax.axis_index(("row", "col"))
    local_rows = voltage.shape[1]
    total_rows = local_rows * device_count
    total_cols = voltage.shape[2]
    local_cols = total_cols // device_count
    total = total_rows * total_cols
    signal = spread(voltage)
    signal = dft_rows(signal, -1.0)
    row_index = jnp.arange(total_rows, dtype=jnp.int32)
    col_index = device * local_cols + jnp.arange(local_cols, dtype=jnp.int32)
    signal = rotate(signal, row_index, col_index, total, -1.0, 1.0)
    signal = collect(signal)
    signal = dft_cols(signal, -1.0)
    turned_phase = jnp.transpose(chirp_phase)
    local_phase = lax.all_to_all(
        turned_phase, ("row", "col"), split_axis=0, concat_axis=1, tiled=True
    )
    signal = complex_product(signal, jnp.cos(local_phase), jnp.sin(local_phase))
    signal = dft_cols(signal, 1.0)
    row_index = device * local_rows + jnp.arange(local_rows, dtype=jnp.int32)
    col_index = jnp.arange(total_cols, dtype=jnp.int32)
    signal = rotate(signal, row_index, col_index, total, 1.0, 1.0 / total)
    signal = spread(signal)
    signal = dft_rows(signal, 1.0)
    signal = collect(signal)
    tap_count = filter_taps.shape[0]
    channel_count = filter_taps.shape[1]
    samples = signal.reshape(2, local_rows * total_cols)
    frame_count = samples.shape[1] // channel_count
    frames = samples.reshape(2, frame_count, channel_count)
    history = passed_along(frames[:, frame_count - tap_count + 1 :, :], ("row", "col"), 1)
    extended = jnp.concatenate([history, frames], axis=1)
    turned = jnp.transpose(extended, (0, 2, 1))
    weighted = jnp.zeros((2, channel_count, frame_count), jnp.float32)
    for tap_delay in range(tap_count):
        offset = tap_count - 1 - tap_delay
        weighted = (
            weighted
            + filter_taps[tap_delay][None, :, None] * turned[:, :, offset : offset + frame_count]
        )
    return dft_rows(weighted, -1.0)


def solution(mesh):
    in_specs = (P(None, ("row", "col"), None), P(("row", "col"), None), P())
    out_specs = P(None, None, ("row", "col"))
    return jax.shard_map(local, mesh=mesh, in_specs=in_specs, out_specs=out_specs, check_vma=False)
```

profile of v0, /device:TPU:6, one launch (start us, length us, event | category | flops | bytes accessed | tf_op | source)
XLA Modules:
  0.0 2393.4 jit_solution(8709069159866349502)
XLA Ops:
  0.0 24.9 %copy.169 = f32[2,128,16384]{1,0,2:T(2,128)} copy(f32[2,128,16384]{2,1,0:T(8,128)} %param.3) | data formatting | bytes 33554432 | tf_op args[0]
  40.1 370.0 %all-to-all-done = f32[2,128,16384]{1,0,2:T(2,128)} async-done(((f32[2,128,16384]{1,0,2:T(2,128)}), f32[2,128,16384]{1,0,2:T(2,128)}, u32[]{:S(2)}, u32[]{:S(2)}) %all-to-all-start) | async-done | bytes 16777248 | tf_op jit(solution)/shard_map/all_to_all | solution.py:83
  414.6 20.2 copy.234
  434.8 21.7 fusion.71
  466.8 28.9 %fusion.59 = f32[2,128,32,512]{3,1,2,0:T(8,128)S(1)} fusion(f32[2,32,128,512]{3,1,2,0:T(8,128)S(1)} %pad_maximum_fusion, f32[1,128,2,128]{1,3,0,2:T(8,128)S(1)} %get-tuple-element.30, f32[1,128,2,128]{1,3,0,2:T(8,128)S(1)} %get-tuple-element.29), kind=kOutput, calls=%fused_computation.103 | convolution fusion | flops 12884967424 | bytes 33816576 | tf_op jit(solution)/shard_map/cbdq,ckbm->dqkm/dot_general | solution.py:53
  519.2 36.9 %fusion.51 = (f32[1,4096,512]{2,1,0:T(8,128)S(1)}, f32[1,4096,512]{2,1,0:T(8,128)S(1)}) fusion(f32[1,128,32,512]{3,2,1,0:T(8,128)S(1)} %copy.173, f32[1,128,32,512]{3,2,1,0:T(8,128)S(1)} %copy.172, s32[512]{0:T(512)S(1)} %iota_add_fusion), kind=kLoop, calls=%fused_computation.77 | loop fusion | flops 41943040 | bytes 33556480 | tf_op jit(solution)/shard_map/sub | solution.py:28
  557.9 32.2 %copy.174 = f32[2,4096,512]{2,0,1:T(2,128)} copy(f32[2,4096,512]{2,1,0:T(8,128)S(1)} %pad_maximum_fusion.1) | data formatting | bytes 33554432 | tf_op jit(solution)/shard_map/stack | solution.py:30
  607.9 31.5 %sine_bitcast_fusion = (f32[128,32,512]{2,0,1:T(8,128)}, f32[128,32,512]{2,0,1:T(8,128)}) fusion(f32[32,128,512]{2,1,0:T(8,128)} %all-to-all-done.2), kind=kLoop, calls=%fused_computation.93 | loop fusion | bytes 25165824 | tf_op jit(solution)/shard_map/sin | solution.py:109
  676.1 309.5 %all-to-all-done.1 = f32[2,4096,512]{2,0,1:T(2,128)} async-done(((f32[2,4096,512]{2,0,1:T(2,128)}), f32[2,4096,512]{2,0,1:T(2,128)}, u32[]{:S(2)}, u32[]{:S(2)}) %all-to-all-start.1) | async-done | bytes 16777248 | tf_op jit(solution)/shard_map/all_to_all | solution.py:87
  999.7 17.5 copy.176
  1017.2 18.1 copy.211
  1035.3 17.1 convolution_bitcast_fusion
  1059.4 31.5 %fusion.36 = f32[2,128,128,128]{2,3,0,1:T(8,128)} fusion(f32[1,128,128,128]{2,3,0,1:T(8,128)} %get-tuple-element.14, f32[1,128,128,128]{2,3,0,1:T(8,128)} %get-tuple-element.13, f32[1,128,2,128]{1,3,0,2:T(8,128)S(1)} %get-tuple-element.30, f32[1,128,2,128]{1,3,0,2:T(8,128)S(1)} %get-tuple-element.29), kind=kOutput, calls=%fused_computation.59 | convolution fusion | flops 12889161728 | bytes 33816576 | tf_op jit(solution)/shard_map/cbdq,cmkb->dmqk/dot_general | solution.py:70
  1090.9 19.0 multiply_subtract_fusion.3
  1109.8 17.3 fusion.37
  1134.3 31.7 %fusion.40 = f32[2,128,128,128]{2,3,0,1:T(8,128)S(1)} fusion(f32[1,128,128,128]{2,3,0,1:T(8,128)} %get-tuple-element.12, f32[1,128,128,128]{2,3,0,1:T(8,128)} %get-tuple-element.11, f32[1,128,2,128]{1,3,2,0:T(8,128)S(1)} %get-tuple-element.28, f32[1,128,2,128]{1,3,2,0:T(8,128)S(1)} %get-tuple-element.27), kind=kOutput, calls=%fused_computation.61 | convolution fusion | flops 12889161728 | bytes 33816576 | tf_op jit(solution)/shard_map/cbdq,cmkb->dmqk/dot_general | solution.py:70
  1191.5 36.6 %fusion.49 = (f32[1,128,16384]{1,2,0:T(8,128)S(1)}, f32[1,128,16384]{1,2,0:T(8,128)S(1)}) fusion(f32[1,128,128,128]{1,3,2,0:T(8,128)} %copy.192, f32[1,128,128,128]{1,3,2,0:T(8,128)} %copy.191, s32[128]{0:T(128)S(1)} %iota_add_fusion.1), kind=kLoop, calls=%fused_computation.71 | loop fusion | flops 46137344 | bytes 33554944 | tf_op jit(solution)/shard_map/sub | solution.py:28
  1229.2 61.7 %copy.193 = f32[2,128,16384]{1,0,2:T(2,128)} copy(f32[2,128,16384]{1,2,0:T(8,128)S(1)} %pad_maximum_fusion.2) | data formatting | bytes 33554432 | tf_op jit(solution)/shard_map/stack | solution.py:30
  1295.5 377.9 %all-to-all-done.3 = f32[2,128,16384]{1,0,2:T(2,128)} async-done(((f32[2,128,16384]{1,0,2:T(2,128)}), f32[2,128,16384]{1,0,2:T(2,128)}, u32[]{:S(2)}, u32[]{:S(2)}) %all-to-all-start.3) | async-done | bytes 16777248 | tf_op jit(solution)/shard_map/all_to_all | solution.py:83
  1673.4 20.1 copy.247
  1693.4 21.7 fusion.74
  1725.4 28.9 %fusion.62 = f32[2,128,32,512]{3,1,2,0:T(8,128)S(1)} fusion(f32[2,32,128,512]{3,1,2,0:T(8,128)S(1)} %pad_maximum_fusion.3, f32[1,128,2,128]{1,3,2,0:T(8,128)S(1)} %get-tuple-element.28, f32[1,128,2,128]{1,3,2,0:T(8,128)S(1)} %get-tuple-element.27), kind=kOutput, calls=%fused_computation.104 | convolution fusion | flops 12884967424 | bytes 33816576 | tf_op jit(solution)/shard_map/cbdq,ckbm->dqkm/dot_general | solution.py:53
  1754.3 20.1 copy.198
  1774.4 28.6 %copy.199 = f32[2,4096,512]{2,0,1:T(2,128)} copy(f32[2,4096,512]{2,1,0:T(8,128)} %bitcast.229) | data formatting | bytes 33554432 | tf_op jit(solution)/shard_map/reshape | solution.py:56
  1807.3 377.8 %all-to-all-done.4 = f32[2,4096,512]{2,0,1:T(2,128)} async-done(((f32[2,4096,512]{2,0,1:T(2,128)}), f32[2,4096,512]{2,0,1:T(2,128)}, u32[]{:S(2)}, u32[]{:S(2)}) %all-to-all-start.4) | async-done | bytes 16777248 | tf_op jit(solution)/shard_map/all_to_all | solution.py:87
  2185.1 17.8 copy.279
  2202.9 19.2 reshape_reshape.3
  2240.3 50.0 %fusion = f32[2,1024,2048]{1,2,0:T(8,128)} fusion(f32[2,1024,2055]{1,2,0:T(8,128)} %maximum_bitcast_fusion, f32[1024]{0:T(1024)S(1)} %bitcast.241, f32[1024]{0:T(1024)S(1)} %bitcast.242, f32[1024]{0:T(1024)S(1)} %bitcast.236, f32[1024]{0:T(1024)S(1)} %bitcast.237, f32[1024]{0:T(1024)S(1)} %bitcast.238, f32[1024]{0:T(1024)S(1)} %bitcast.239, ...), kind=kLoop, calls=%fused_computation.2 | loop fusion | flops 62914560 | bytes 151027712 | tf_op jit(solution)/shard_map/add | solution.py:129
  2290.3 17.3 copy.201
  2307.7 32.0 %fusion.65 = f32[2,8,128,2048]{3,1,2,0:T(8,128)} fusion(f32[2,8,128,2048]{3,2,1,0:T(8,128)} %bitcast.231, f32[1,8,2,8]{1,3,0,2:T(8,128)S(1)} %copy.167, f32[1,8,2,8]{1,3,0,2:T(8,128)S(1)} %copy.166), kind=kOutput, calls=%fused_computation.105 | convolution fusion | flops 805306624 | bytes 33555456 | tf_op jit(solution)/shard_map/cadk,cabm->dkbm/dot_general | solution.py:48
  2349.0 23.7 fusion.68
  2372.7 20.2 copy.278
  (70 shorter events, 210.8 us)
Async XLA Ops:
  24.9 385.2 %all-to-all-start = ((f32[2,128,16384]{1,0,2:T(2,128)}), f32[2,128,16384]{1,0,2:T(2,128)}, u32[]{:S(2)}, u32[]{:S(2)}) async-start(f32[2,128,16384]{1,0,2:T(2,128)} %copy.169), calls=%async_computation | async-start | bytes 33554432 | tf_op jit(solution)/shard_map/all_to_all | solution.py:83
  410.1 191.6 %all-to-all-start.2 = ((f32[32,128,512]{2,1,0:T(8,128)}), f32[32,128,512]{2,1,0:T(8,128)}, u32[]{:S(2)}, u32[]{:S(2)}) async-start(f32[32,128,512]{2,1,0:T(8,128)} %bitcast.232), calls=%async_computation.2 | async-start | bytes 16777216 | tf_op jit(solution)/shard_map/all_to_all | solution.py:106
  414.6 644.8 %copy-start = (f32[1,128,2,128]{1,3,0,2:T(8,128)}, f32[1,128,2,128]{1,3,0,2:T(8,128)S(1)}, u32[]{:S(2)}) copy-start(f32[1,128,2,128]{1,3,0,2:T(8,128)S(1)} %get-tuple-element.29) | copy-start | bytes 393220
  414.6 644.8 %copy-start.2 = (f32[1,128,2,128]{1,3,0,2:T(8,128)}, f32[1,128,2,128]{1,3,0,2:T(8,128)S(1)}, u32[]{:S(2)}) copy-start(f32[1,128,2,128]{1,3,0,2:T(8,128)S(1)} %get-tuple-element.30) | copy-start | bytes 393220
  601.7 383.8 %all-to-all-start.1 = ((f32[2,4096,512]{2,0,1:T(2,128)}), f32[2,4096,512]{2,0,1:T(2,128)}, u32[]{:S(2)}, u32[]{:S(2)}) async-start(f32[2,4096,512]{2,0,1:T(2,128)} %copy.174), calls=%async_computation.1 | async-start | bytes 33554432 | tf_op jit(solution)/shard_map/all_to_all | solution.py:87
  1291.0 382.4 %all-to-all-start.3 = ((f32[2,128,16384]{1,0,2:T(2,128)}), f32[2,128,16384]{1,0,2:T(2,128)}, u32[]{:S(2)}, u32[]{:S(2)}) async-start(f32[2,128,16384]{1,0,2:T(2,128)} %copy.193), calls=%async_computation.3 | async-start | bytes 33554432 | tf_op jit(solution)/shard_map/all_to_all | solution.py:83
  1803.0 4.2 copy-start.4
  1803.0 382.1 %all-to-all-start.4 = ((f32[2,4096,512]{2,0,1:T(2,128)}), f32[2,4096,512]{2,0,1:T(2,128)}, u32[]{:S(2)}, u32[]{:S(2)}) async-start(f32[2,4096,512]{2,0,1:T(2,128)} %copy.199), calls=%async_computation.4 | async-start | bytes 33554432 | tf_op jit(solution)/shard_map/all_to_all | solution.py:87
  2222.9 5.6 collective-permute-start
  2346.9 2.0 copy-start.1
  2346.9 2.0 copy-start.3
where the time goes:
time: 2410 us; the launch traced here: 2390 us
  waiting for transfers between devices  1450 us (60%)
  local copies, waits for them, and re-layouts  460 us (19%)
  matrix products  255 us (11%)
  other arithmetic  204 us (8%)
  starting transfers between devices  24.3 us (1%)
    all_to_all x2, waiting for transfers between devices, spread(): lax.all_to_all(values, ('row', 'col'), split_axis=2, concat_axis=1, tiled...  748 us
    all_to_all x2, waiting for transfers between devices, collect(): lax.all_to_all(values, ('row', 'col'), split_axis=1, concat_axis=2, tiled...  687 us
    sub x8, other arithmetic, complex_product(): real_part = values[0] * cos_part - values[1] * sin_part  128 us
    another operation x2, local copies, waits for them, and re-layouts, complex_product(): return jnp.stack([real_part, imag_part])  94 us
    dot_general x3, matrix products, dft_rows(): jnp.einsum('cbdq,ckbm->dqkm', dft_table(inner_radix, direction), partial_...  81.5 us
    dot_general x3, matrix products, dft_rows(): jnp.einsum('cadk,cabm->dkbm', dft_table(outer_radix, direction), blocked,...  75.5 us
    dot_general x2, matrix products, dft_cols(): jnp.einsum('cbdq,cmkb->dmqk', dft_table(inner_radix, direction), partial_...  63.2 us
    add x1, other arithmetic, local(): weighted + filter_taps[tap_delay][None, :, None] * turned[:, :, offset:of...  50 us
  transfers between devices with their start and end apart: 6, of which 6 were waited for; matrix products, arithmetic and copies ran while one was open for 11% of the time, Pallas kernels for 0%

commit v1 on v0

--- a/solution.py
+++ b/solution.py
@@ -1,3 +1,4 @@
+import functools
 import math
 import jax
 import jax.numpy as jnp
@@ -5,6 +6,19 @@
 from jax.sharding import PartitionSpec as P
 
 precise = lax.Precision.HIGHEST
+
+
+def start_counts_all(u_in, axis_tag):
+    tall = jnp.concatenate(
+        lax.all_to_all(
+            jnp.stack(jnp.split(u_in, lax.axis_size(axis_tag), 1), axis=0), axis_tag, 0, 0
+        ),
+        2,
+    )
+    return tall
+
+
+convert_digits = functools.partial(start_counts_all, axis_tag=("row", "col"))
 
 
 def passed_along(block, axis, distance):
@@ -84,7 +98,7 @@
 
 
 def collect(values):
-    return lax.all_to_all(values, ("row", "col"), split_axis=1, concat_axis=2, tiled=True)
+    return convert_digits(values)
 
 
 def local(voltage, chirp_phase, filter_taps):

time: 2410 us -> 2390 us (level)
  local copies, waits for them, and re-layouts: 460 us -> 408 us
  other arithmetic: 204 us -> 229 us
    all_to_all x3 -> x0, local copies, waits for them, and re-layouts: 49.4 us -> none  [collect(): lax.all_to_all(values, ('row', 'col'), split_axis=1, concat_axis=2, tiled...]
    another operation x2 -> x1, local copies, waits for them, and re-layouts: 94 us -> 61.7 us  [complex_product(): return jnp.stack([real_part, imag_part])]
    unnamed x12 -> x47, local copies, waits for them, and re-layouts: 34 us -> 59.7 us
    unnamed x0 -> x31, other arithmetic: none -> 25.7 us
  transfers between devices with their start and end apart: 6 -> 6, of which waited for: 6 -> 6; matrix products, arithmetic and copies ran while one was open for 11% -> 10% of each run, Pallas kernels for 0% -> 0%
where the time goes in v1:
time: 2390 us; the launch traced here: 2370 us
  waiting for transfers between devices  1460 us (61%)
  local copies, waits for them, and re-layouts  408 us (17%)
  matrix products  255 us (11%)
  other arithmetic  229 us (10%)
  starting transfers between devices  24.3 us (1%)
    all_to_all x2, waiting for transfers between devices, spread(): lax.all_to_all(values, ('row', 'col'), split_axis=2, concat_axis=1, tiled...  748 us
    all_to_all x2, waiting for transfers between devices, start_counts_all(): lax.all_to_all(jnp.stack(jnp.split(u_in, lax.axis_size(axis_tag), 1), axi...  687 us
    sub x8, other arithmetic, complex_product(): real_part = values[0] * cos_part - values[1] * sin_part  128 us
    dot_general x3, matrix products, dft_rows(): jnp.einsum('cbdq,ckbm->dqkm', dft_table(inner_radix, direction), partial_...  81.5 us
    dot_general x3, matrix products, dft_rows(): jnp.einsum('cadk,cabm->dkbm', dft_table(outer_radix, direction), blocked,...  75.5 us
    dot_general x2, matrix products, dft_cols(): jnp.einsum('cbdq,cmkb->dmqk', dft_table(inner_radix, direction), partial_...  63.2 us
    another operation x1, local copies, waits for them, and re-layouts, complex_product(): return jnp.stack([real_part, imag_part])  61.7 us
    unnamed x47, local copies, waits for them, and re-layouts  59.7 us
  transfers between devices with their start and end apart: 6, of which 6 were waited for; matrix products, arithmetic and copies ran while one was open for 10% of the time, Pallas kernels for 0%

profile of v1, /device:TPU:6, one launch (start us, length us, event | category | flops | bytes accessed | tf_op | source)
XLA Modules:
  0.0 2374.4 jit_solution(6781259854117423444)
XLA Ops:
  0.0 24.9 %copy.128 = f32[2,128,16384]{1,0,2:T(2,128)} copy(f32[2,128,16384]{2,1,0:T(8,128)} %param.3) | data formatting | bytes 33554432 | tf_op args[0]
  40.1 370.0 %all-to-all-done = f32[2,128,16384]{1,0,2:T(2,128)} async-done(((f32[2,128,16384]{1,0,2:T(2,128)}), f32[2,128,16384]{1,0,2:T(2,128)}, u32[]{:S(2)}, u32[]{:S(2)}) %all-to-all-start) | async-done | bytes 16777248 | tf_op jit(solution)/shard_map/all_to_all | solution.py:97
  414.6 20.2 copy.190
  434.8 21.7 fusion.71
  466.8 28.9 %fusion.59 = f32[2,128,32,512]{3,1,2,0:T(8,128)S(1)} fusion(f32[2,32,128,512]{3,1,2,0:T(8,128)S(1)} %pad_maximum_fusion, f32[1,128,2,128]{1,3,0,2:T(8,128)S(1)} %get-tuple-element.30, f32[1,128,2,128]{1,3,0,2:T(8,128)S(1)} %get-tuple-element.29), kind=kOutput, calls=%fused_computation.163 | convolution fusion | flops 12884967424 | bytes 33816576 | tf_op jit(solution)/shard_map/cbdq,ckbm->dqkm/dot_general | solution.py:67
  519.2 36.9 %fusion.51 = (f32[1,4096,512]{2,1,0:T(8,128)S(1)}, f32[1,4096,512]{2,1,0:T(8,128)S(1)}) fusion(f32[1,128,32,512]{3,2,1,0:T(8,128)S(1)} %copy.132, f32[1,128,32,512]{3,2,1,0:T(8,128)S(1)} %copy.131, s32[512]{0:T(512)S(1)} %iota_add_fusion), kind=kLoop, calls=%fused_computation.137 | loop fusion | flops 41943040 | bytes 33556480 | tf_op jit(solution)/shard_map/sub | solution.py:42
  582.6 19.1 all-to-all-done.2
  607.9 31.5 %sine_bitcast_fusion = (f32[128,32,512]{2,0,1:T(8,128)}, f32[128,32,512]{2,0,1:T(8,128)}) fusion(f32[32,128,512]{2,1,0:T(8,128)} %all-to-all-done.2), kind=kLoop, calls=%fused_computation.153 | loop fusion | bytes 25165824 | tf_op jit(solution)/shard_map/sin | solution.py:123
  676.1 309.5 %all-to-all-done.1 = f32[32,2,128,512]{3,2,1,0:T(8,128)} async-done(((f32[32,2,128,512]{3,2,1,0:T(8,128)}), f32[32,2,128,512]{3,2,1,0:T(8,128)}, u32[]{:S(2)}, u32[]{:S(2)}) %all-to-all-start.1) | async-done | bytes 16777248 | tf_op jit(solution)/shard_map/all_to_all | solution.py:13
  985.5 17.4 copy.133
  1002.9 18.2 copy.167
  1021.1 17.1 convolution_bitcast_fusion
  1045.2 31.5 %fusion.36 = f32[2,128,128,128]{2,3,0,1:T(8,128)} fusion(f32[1,128,128,128]{2,3,0,1:T(8,128)} %get-tuple-element.14, f32[1,128,128,128]{2,3,0,1:T(8,128)} %get-tuple-element.13, f32[1,128,2,128]{1,3,0,2:T(8,128)S(1)} %copy-done.4, f32[1,128,2,128]{1,3,0,2:T(8,128)S(1)} %copy-done.1), kind=kOutput, calls=%fused_computation.119 | convolution fusion | flops 12889161728 | bytes 33816576 | tf_op jit(solution)/shard_map/cbdq,cmkb->dmqk/dot_general | solution.py:84
  1076.6 18.9 multiply_subtract_fusion.3
  1095.6 17.3 fusion.37
  1120.0 31.7 %fusion.40 = f32[2,128,128,128]{2,3,0,1:T(8,128)S(1)} fusion(f32[1,128,128,128]{2,3,0,1:T(8,128)} %get-tuple-element.12, f32[1,128,128,128]{2,3,0,1:T(8,128)} %get-tuple-element.11, f32[1,128,2,128]{1,3,2,0:T(8,128)S(1)} %get-tuple-element.28, f32[1,128,2,128]{1,3,2,0:T(8,128)S(1)} %get-tuple-element.27), kind=kOutput, calls=%fused_computation.121 | convolution fusion | flops 12889161728 | bytes 33816576 | tf_op jit(solution)/shard_map/cbdq,cmkb->dmqk/dot_general | solution.py:84
  1177.2 36.6 %fusion.49 = (f32[1,128,16384]{1,2,0:T(8,128)S(1)}, f32[1,128,16384]{1,2,0:T(8,128)S(1)}) fusion(f32[1,128,128,128]{1,3,2,0:T(8,128)} %copy.149, f32[1,128,128,128]{1,3,2,0:T(8,128)} %copy.148, s32[128]{0:T(128)S(1)} %iota_add_fusion.1), kind=kLoop, calls=%fused_computation.131 | loop fusion | flops 46137344 | bytes 33554944 | tf_op jit(solution)/shard_map/sub | solution.py:42
  1214.9 61.7 %copy.150 = f32[2,128,16384]{1,0,2:T(2,128)} copy(f32[2,128,16384]{1,2,0:T(8,128)S(1)} %pad_maximum_fusion.1) | data formatting | bytes 33554432 | tf_op jit(solution)/shard_map/stack | solution.py:44
  1281.2 377.9 %all-to-all-done.3 = f32[2,128,16384]{1,0,2:T(2,128)} async-done(((f32[2,128,16384]{1,0,2:T(2,128)}), f32[2,128,16384]{1,0,2:T(2,128)}, u32[]{:S(2)}, u32[]{:S(2)}) %all-to-all-start.3) | async-done | bytes 16777248 | tf_op jit(solution)/shard_map/all_to_all | solution.py:97
  1659.1 20.1 copy.203
  1679.2 21.7 fusion.74
  1711.1 28.9 %fusion.62 = f32[2,128,32,512]{3,1,2,0:T(8,128)S(1)} fusion(f32[2,32,128,512]{3,1,2,0:T(8,128)S(1)} %pad_maximum_fusion.2, f32[1,128,2,128]{1,3,2,0:T(8,128)S(1)} %get-tuple-element.28, f32[1,128,2,128]{1,3,2,0:T(8,128)S(1)} %get-tuple-element.27), kind=kOutput, calls=%fused_computation.164 | convolution fusion | flops 12884967424 | bytes 33816576 | tf_op jit(solution)/shard_map/cbdq,ckbm->dqkm/dot_general | solution.py:67
  1740.1 17.5 copy.155
  1788.3 377.8 %all-to-all-done.4 = f32[32,2,128,512]{3,2,1,0:T(8,128)} async-done(((f32[32,2,128,512]{3,2,1,0:T(8,128)}), f32[32,2,128,512]{3,2,1,0:T(8,128)}, u32[]{:S(2)}, u32[]{:S(2)}) %all-to-all-start.4) | async-done | bytes 16777248 | tf_op jit(solution)/shard_map/all_to_all | solution.py:13
  2166.1 17.8 copy.156
  2183.9 19.2 reshape_reshape_reshape.3
  2209.5 11.8 maximum_bitcast_fusion
  2221.3 50.0 %fusion = f32[2,1024,2048]{1,2,0:T(8,128)} fusion(f32[2,1024,2055]{1,2,0:T(8,128)} %maximum_bitcast_fusion, f32[1024]{0:T(1024)S(1)} %bitcast.459, f32[1024]{0:T(1024)S(1)} %bitcast.460, f32[1024]{0:T(1024)S(1)} %bitcast.454, f32[1024]{0:T(1024)S(1)} %bitcast.455, f32[1024]{0:T(1024)S(1)} %bitcast.456, f32[1024]{0:T(1024)S(1)} %bitcast.457, ...), kind=kLoop, calls=%fused_computation.64 | loop fusion | flops 62914560 | bytes 151027712 | tf_op jit(solution)/shard_map/add | solution.py:143
  2271.4 17.3 copy.157
  2288.7 32.0 %fusion.65 = f32[2,8,128,2048]{3,1,2,0:T(8,128)} fusion(f32[2,8,128,2048]{3,2,1,0:T(8,128)} %bitcast.449, f32[1,8,2,8]{1,3,0,2:T(8,128)S(1)} %copy.126, f32[1,8,2,8]{1,3,0,2:T(8,128)S(1)} %copy.125), kind=kOutput, calls=%fused_computation.165 | convolution fusion | flops 805306624 | bytes 33555456 | tf_op jit(solution)/shard_map/cadk,cabm->dkbm/dot_general | solution.py:62
  2330.1 23.7 fusion.68
  2353.8 20.2 copy.233
  (134 shorter events, 224.5 us)
Async XLA Ops:
  24.9 385.2 %all-to-all-start = ((f32[2,128,16384]{1,0,2:T(2,128)}), f32[2,128,16384]{1,0,2:T(2,128)}, u32[]{:S(2)}, u32[]{:S(2)}) async-start(f32[2,128,16384]{1,0,2:T(2,128)} %copy.128), calls=%async_computation | async-start | bytes 33554432 | tf_op jit(solution)/shard_map/all_to_all | solution.py:97
  410.1 191.6 %all-to-all-start.2 = ((f32[32,128,512]{2,1,0:T(8,128)}), f32[32,128,512]{2,1,0:T(8,128)}, u32[]{:S(2)}, u32[]{:S(2)}) async-start(f32[32,128,512]{2,1,0:T(8,128)} %bitcast.450), calls=%async_computation.2 | async-start | bytes 16777216 | tf_op jit(solution)/shard_map/all_to_all | solution.py:120
  414.6 52.2 %copy-start = (f32[1,128,2,128]{1,3,0,2:T(8,128)}, f32[1,128,2,128]{1,3,0,2:T(8,128)S(1)}, u32[]{:S(2)}) copy-start(f32[1,128,2,128]{1,3,0,2:T(8,128)S(1)} %get-tuple-element.29) | copy-start | bytes 393220
  414.6 52.2 %copy-start.3 = (f32[1,128,2,128]{1,3,0,2:T(8,128)}, f32[1,128,2,128]{1,3,0,2:T(8,128)S(1)}, u32[]{:S(2)}) copy-start(f32[1,128,2,128]{1,3,0,2:T(8,128)S(1)} %get-tuple-element.30) | copy-start | bytes 393220
  601.7 383.8 %all-to-all-start.1 = ((f32[32,2,128,512]{3,2,1,0:T(8,128)}), f32[32,2,128,512]{3,2,1,0:T(8,128)}, u32[]{:S(2)}, u32[]{:S(2)}) async-start(f32[32,2,128,512]{3,2,1,0:T(8,128)} %fusion.143), calls=%async_computation.1 | async-start | bytes 33554432 | tf_op jit(solution)/shard_map/all_to_all | solution.py:13
  1002.9 18.2 copy-start.1
  1002.9 18.2 copy-start.4
  1276.7 382.4 %all-to-all-start.3 = ((f32[2,128,16384]{1,0,2:T(2,128)}), f32[2,128,16384]{1,0,2:T(2,128)}, u32[]{:S(2)}, u32[]{:S(2)}) async-start(f32[2,128,16384]{1,0,2:T(2,128)} %copy.150), calls=%async_computation.3 | async-start | bytes 33554432 | tf_op jit(solution)/shard_map/all_to_all | solution.py:97
  1784.1 4.2 copy-start.6
  1784.1 382.1 %all-to-all-start.4 = ((f32[32,2,128,512]{3,2,1,0:T(8,128)}), f32[32,2,128,512]{3,2,1,0:T(8,128)}, u32[]{:S(2)}, u32[]{:S(2)}) async-start(f32[32,2,128,512]{3,2,1,0:T(8,128)} %fusion.110), calls=%async_computation.4 | async-start | bytes 33554432 | tf_op jit(solution)/shard_map/all_to_all | solution.py:13
  2204.0 5.6 collective-permute-start
  2328.0 2.0 copy-start.2
  2328.0 2.0 copy-start.5
